TPU v7x, 256 devices: a whole 4x4x8 slice. The times are simulated.
256 devices in a mesh: ens: 4 (over y), fsdp: 16 (over z, core), model: 4 (over x).
Axes of the slice: x: 4, y: 4, z: 8, core: 2. Of those that a mesh axis runs over, the one named last changes fastest.
Arguments:
- weight_gate: bfloat16 [8192, 8192], P(('ens', 'fsdp'), 'model'), parts along dimension 0, may hold values from -0.125 to 0.125
- low_gate: bfloat16 [8192, 32], P(('ens', 'fsdp')), parts along dimension 0, may hold values from -0.125 to 0.125
- high_gate: bfloat16 [128, 8192], P('ens', 'model'), parts along dimension 0, may hold values from -1 to 1
- weight_up: bfloat16 [8192, 8192], P(('ens', 'fsdp'), 'model'), parts along dimension 0, may hold values from -0.125 to 0.125
- low_up: bfloat16 [8192, 32], P(('ens', 'fsdp')), parts along dimension 0, may hold values from -0.125 to 0.125
- high_up: bfloat16 [128, 8192], P('ens', 'model'), parts along dimension 0, may hold values from -1 to 1
- norm_train: float32 [8192], P(('ens', 'fsdp', 'model')), parts along dimension 0, may hold values from 0.25 to 1.75
- norm_step: float32 [8192], P(('ens', 'fsdp', 'model')), parts along dimension 0, may hold values from -0.3 to 0.3
Outputs:
- final_gate: bfloat16 [32768, 2048], P(('ens', 'model')), parts along dimension 0
- final_up: bfloat16 [32768, 2048], P(('ens', 'model')), parts along dimension 0
- serve_norm: bfloat16 [8192], P('ens'), parts along dimension 0
There are 4 independent parts, one for each index of `ens`. A program takes and returns all parts, laid end to end along the dimension named above; each array names one. Nothing has to cross between parts.
All inputs are finite; a program needn't handle non-finite values.
Results may differ from a plain program's by a relative error of at most 0.001.
Values may be sent and summed in bfloat16 or wider, within the bound.
A program may use at most 128 MiB of HBM per device.

v0:
```python
import jax
import jax.numpy as jnp
from jax import lax
from jax.sharding import PartitionSpec as P

mix_rate = 2.0


def sent_to_all(shard, axis):
    copies = jnp.broadcast_to(shard, (lax.axis_size(axis), *shard.shape))
    return lax.all_to_all(copies, axis, split_axis=0, concat_axis=0, tiled=True)


def joined_along(blocks, dim):
    shape = list(blocks.shape[1:])
    shape[dim] *= blocks.shape[0]
    return jnp.moveaxis(blocks, 0, dim).reshape(shape)


def gather_directly(shard, axis, dim):
    blocks = sent_to_all(shard, axis)
    return joined_along(blocks, dim)


def body(weight_gate, low_gate, high_gate, weight_up, low_up, high_up, norm_train, norm_step):
    result_gate = weight_gate.astype(jnp.float32) + mix_rate * jnp.dot(
        low_gate, high_gate, preferred_element_type=jnp.float32
    )
    result_up = weight_up.astype(jnp.float32) + mix_rate * jnp.dot(
        low_up, high_up, preferred_element_type=jnp.float32
    )
    narrow_gate, narrow_up = (result_gate.astype(jnp.bfloat16), result_up.astype(jnp.bfloat16))
    final_gate, final_up = (
        lax.all_gather(narrow_gate, "fsdp", axis=0, tiled=True),
        lax.all_gather(narrow_up, "fsdp", axis=0, tiled=True),
    )
    final_gate, final_up = (final_gate.T, final_up.T)
    serve_norm = gather_directly(
        (norm_train + norm_step).astype(jnp.bfloat16), ("fsdp", "model"), 0
    )
    return (final_gate, final_up, serve_norm)


def solution(mesh):
    return jax.shard_map(
        body,
        mesh=mesh,
        in_specs=(
            P(("ens", "fsdp"), "model"),
            P(("ens", "fsdp"), None),
            P("ens", "model"),
            P(("ens", "fsdp"), "model"),
            P(("ens", "fsdp"), None),
            P("ens", "model"),
            P(("ens", "fsdp", "model")),
            P(("ens", "fsdp", "model")),
        ),
        out_specs=(P(("ens", "model"), None), P(("ens", "model"), None), P("ens")),
        check_vma=False,
    )
```

profile of v0, /device:TPU:1, one launch (start us, length us, event | category | flops | bytes accessed | tf_op | source)
XLA Modules:
  0.0 146.5 jit_solution(759625118744581745)
XLA Ops:
  7.2 0.0 copy-start
  7.2 0.0 all-gather.3.cloned.1.call-start
  7.2 0.8 copy-done
  8.1 2.2 %fusion.3 = bf16[128,2048]{1,0:T(8,128)(2,1)} fusion(bf16[128,32]{0,1:T(8,128)(2,1)} %param.9, bf16[32,2048]{1,0:T(8,128)(2,1)S(1)} %copy-done, bf16[128,2048]{1,0:T(8,128)(2,1)} %param.8), kind=kOutput, calls=%fused_computation.5 | convolution fusion | flops 17825792 | bytes 1187840 | tf_op jit(solution)/shard_map/dot_general | solution.py:26
  10.2 0.0 all-gather.3.cloned.1.call-update
  10.3 0.0 all-gather.5.cloned.1.call-start
  10.3 2.2 %fusion.2 = bf16[128,2048]{1,0:T(8,128)(2,1)} fusion(bf16[128,32]{0,1:T(8,128)(2,1)} %param.12, bf16[32,2048]{1,0:T(8,128)(2,1)} %param.13, bf16[128,2048]{1,0:T(8,128)(2,1)} %param.11), kind=kOutput, calls=%fused_computation.4 | convolution fusion | flops 17825792 | bytes 1187840 | tf_op jit(solution)/shard_map/dot_general | solution.py:29
  12.6 0.0 all-gather.5.cloned.1.call-update
  12.6 0.7 add_convert_fusion
  13.3 22.0 %all_to_all.6 = bf16[64,1,32]{2,1,0:T(2,128)(2,1)S(1)} all-to-all(bf16[64,1,32]{2,1,0:T(2,128)(2,1)S(1)} %broadcast_in_dim.3), channel_id=1, replica_groups=mesh['ens'=4,'fsdp'=16,'model'=4] {'fsdp','model'}, dimensions={0} | all-to-all | bytes 8192 | tf_op jit(solution)/shard_map/all_to_all | solution.py:11
  35.3 0.1 reduce
  35.4 0.7 reshape.14
  36.1 35.1 %all-gather.3.cloned.1.call-done = bf16[2048,2048]{1,0:T(8,128)(2,1)} async-done(((bf16[128,2048]{1,0:T(8,128)(2,1)}), bf16[2048,2048]{1,0:T(8,128)(2,1)}) %all-gather.3.cloned.1.call-update) | async-done | bytes 8388624 | tf_op jit(solution)/shard_map/all_gather | solution.py:34
  71.2 12.2 %copy.15 = bf16[2048,2048]{1,0:T(8,128)(2,1)} copy(bf16[2048,2048]{0,1:T(8,128)(2,1)} %bitcast.6) | data formatting | bytes 16777216
  83.4 44.0 %all-gather.5.cloned.1.call-done = bf16[2048,2048]{1,0:T(8,128)(2,1)} async-done(((bf16[128,2048]{1,0:T(8,128)(2,1)}), bf16[2048,2048]{1,0:T(8,128)(2,1)}) %all-gather.5.cloned.1.call-update) | async-done | bytes 8388624 | tf_op jit(solution)/shard_map/all_gather | solution.py:35
  127.4 12.2 %copy.16 = bf16[2048,2048]{1,0:T(8,128)(2,1)} copy(bf16[2048,2048]{0,1:T(8,128)(2,1)} %bitcast.7) | data formatting | bytes 16777216
  (1 shorter events, 0.0 us)
Async XLA Ops:
  7.2 0.9 copy-start
  7.2 64.0 %all-gather.3.cloned.1.call-start = ((), (), s32[]{:S(2)}) async-start(), calls=%async_computation.1 | async-start | bytes 8912896 | tf_op jit(solution)/shard_map/all_gather | solution.py:34
  10.3 117.2 %all-gather.5.cloned.1.call-start = ((), (), s32[]{:S(2)}) async-start(), calls=%async_computation.2 | async-start | bytes 8912896 | tf_op jit(solution)/shard_map/all_gather | solution.py:35
Sparse Core Ops, SparseCore 0:
  10.4 60.7 all-gather.2
  73.0 54.3 all-gather.4
where the time goes:
time: 147 us; the launch traced here: 146 us
  waiting for transfers between devices  79.1 us (54%)
  local copies, waits for them, and re-layouts  26 us (18%)
  blocking collectives  22 us (15%)
  between operations  14.1 us (10%)
  matrix products  4.42 us (3%)
    all_gather x1, waiting for transfers between devices, body(): lax.all_gather(narrow_up, 'fsdp', axis=0, tiled=True)  44 us
    all_gather x1, waiting for transfers between devices, body(): lax.all_gather(narrow_gate, 'fsdp', axis=0, tiled=True)  35.1 us
    unnamed x4, local copies, waits for them, and re-layouts  25.3 us
    all_to_all x1, blocking collectives, sent_to_all(): return lax.all_to_all(copies, axis, split_axis=0, concat_axis=0, tiled=True)  22 us
  transfers between devices with their start and end apart: 2, of which 2 were waited for; matrix products, arithmetic and copies ran while one was open for 11% of the time, Pallas kernels for 0%

commit v1 on v0

--- a/solution.py
+++ b/solution.py
@@ -4,6 +4,27 @@
 from jax.sharding import PartitionSpec as P
 
 mix_rate = 2.0
+
+
+def ring_gather(shard, axis, dim):
+    devices, here, rows = (lax.axis_size(axis), lax.axis_index(axis), shard.shape[dim])
+    upward = [(i, (i + 1) % devices) for i in range(devices)]
+    left = [(i, (i - 1) % devices) for i in range(devices)]
+    result = jnp.zeros((*shard.shape[:dim], devices * rows, *shard.shape[dim + 1 :]), shard.dtype)
+    result = lax.dynamic_update_slice_in_dim(result, shard, here * rows, axis=dim)
+    from_left = from_right = shard
+    middle = devices // 2
+    for step in range(1, middle + 1):
+        from_left = lax.ppermute(from_left, axis, upward)
+        result = lax.dynamic_update_slice_in_dim(
+            result, from_left, (here - step) % devices * rows, axis=dim
+        )
+        if step < devices - middle:
+            from_right = lax.ppermute(from_right, axis, left)
+            result = lax.dynamic_update_slice_in_dim(
+                result, from_right, (here + step) % devices * rows, axis=dim
+            )
+    return result
 
 
 def sent_to_all(shard, axis):
@@ -31,7 +52,7 @@
     )
     narrow_gate, narrow_up = (result_gate.astype(jnp.bfloat16), result_up.astype(jnp.bfloat16))
     final_gate, final_up = (
-        lax.all_gather(narrow_gate, "fsdp", axis=0, tiled=True),
+        ring_gather(narrow_gate, "fsdp", 0),
         lax.all_gather(narrow_up, "fsdp", axis=0, tiled=True),
     )
     final_gate, final_up = (final_gate.T, final_up.T)

time: 147 us -> 145 us (0.986)
  the two profiles are of different devices: /device:TPU:1 before, /device:TPU:10 now
where the time goes in v1:
time: 145 us
  waiting for transfers between devices  52.1 us (36%)
  local copies, waits for them, and re-layouts  40.6 us (28%)
  starting transfers between devices  33.5 us (23%)
  between operations  14.2 us (10%)
  matrix products  3.68 us (3%)
    ppermute x8, waiting for transfers between devices, ring_gather(): from_left = lax.ppermute(from_left, axis, upward)  50.8 us
    ppermute x7, starting transfers between devices, ring_gather(): from_right = lax.ppermute(from_right, axis, left)  23.1 us
    unnamed x5, local copies, waits for them, and re-layouts  13.1 us
    all_to_all x1, starting transfers between devices, sent_to_all(): return lax.all_to_all(copies, axis, split_axis=0, concat_axis=0, tiled=True)  10.2 us
    dynamic_update_slice x8, local copies, waits for them, and re-layouts, ring_gather(): lax.dynamic_update_slice_in_dim(result, from_left, (here - step) % device...  6.64 us
    dynamic_update_slice x7, local copies, waits for them, and re-layouts, ring_gather(): lax.dynamic_update_slice_in_dim(result, from_right, (here + step) % devic...  5.8 us
    ppermute x8, local copies, waits for them, and re-layouts, ring_gather(): from_left = lax.ppermute(from_left, axis, upward)  5.27 us
    broadcast_in_dim x1, local copies, waits for them, and re-layouts, ring_gather(): jnp.zeros((*shard.shape[:dim], devices * rows, *shard.shape[dim + 1:]), s...  4.46 us
  transfers between devices with their start and end apart: 17, of which 10 were waited for; matrix products, arithmetic and copies ran while one was open for 21% of the time, Pallas kernels for 0%

profile of v1, /device:TPU:10, one launch (start us, length us, event | category | flops | bytes accessed | tf_op | source)
XLA Modules:
  0.0 144.8 jit_solution(13017764923984456552)
XLA Ops:
  8.1 2.2 %fusion.2 = bf16[128,2048]{1,0:T(8,128)(2,1)} fusion(bf16[128,32]{0,1:T(8,128)(2,1)} %param.12, bf16[32,2048]{1,0:T(8,128)(2,1)S(1)} %copy-done, bf16[128,2048]{1,0:T(8,128)(2,1)} %param.11), kind=kOutput, calls=%fused_computation.4 | convolution fusion | flops 17825792 | bytes 1187840 | tf_op jit(solution)/shard_map/dot_general | solution.py:50
  10.3 1.5 %fusion.3 = bf16[128,2048]{1,0:T(8,128)(2,1)S(1)} fusion(bf16[128,32]{0,1:T(8,128)(2,1)} %param.9, bf16[32,2048]{1,0:T(8,128)(2,1)} %param.10, bf16[128,2048]{1,0:T(8,128)(2,1)} %param.8), kind=kOutput, calls=%fused_computation.5 | convolution fusion | flops 17825792 | bytes 1187840 | tf_op jit(solution)/shard_map/dot_general | solution.py:47
  11.8 5.3 %collective-permute-start.1 = (bf16[128,2048]{1,0:T(8,128)(2,1)S(1)}, bf16[128,2048]{1,0:T(8,128)(2,1)S(1)}, u32[]{:S(2)}, u32[]{:S(2)}) collective-permute-start(bf16[128,2048]{1,0:T(8,128)(2,1)S(1)} %fusion.3), channel_id=1, source_target_pairs={{0,60},{4,0},{8,4},{12,8},{16,12},{20,16},{24,20},{28,24},{32,28},... | collective-permute-start | bytes 1572872 | tf_op jit(solution)/shard_map/ppermute | solution.py:23
  17.1 6.8 %collective-permute-done = bf16[128,2048]{1,0:T(8,128)(2,1)S(1)} collective-permute-done((bf16[128,2048]{1,0:T(8,128)(2,1)S(1)}, bf16[128,2048]{1,0:T(8,128)(2,1)S(1)}, u32[]{:S(2)}, u32[]{:S(2)}) %collective-permute-start) | collective-permute-done | bytes 524320 | tf_op jit(solution)/shard_map/ppermute | solution.py:18
  24.0 3.0 %collective-permute-start.3 = (bf16[128,2048]{1,0:T(8,128)(2,1)S(1)}, bf16[128,2048]{1,0:T(8,128)(2,1)S(1)}, u32[]{:S(2)}, u32[]{:S(2)}) collective-permute-start(bf16[128,2048]{1,0:T(8,128)(2,1)S(1)} %collective-permute-done.1), channel_id=1, source_target_pairs={{0,60},{4,0},{8,4},{12,8},{16,12},{20,16},{24,20},{28,24},{32,28},... | collective-permute-start | bytes 1572872 | tf_op jit(solution)/shard_map/ppermute | solution.py:23
  26.9 18.0 %collective-permute-done.2 = bf16[128,2048]{1,0:T(8,128)(2,1)} collective-permute-done((bf16[128,2048]{1,0:T(8,128)(2,1)S(1)}, bf16[128,2048]{1,0:T(8,128)(2,1)}, u32[]{:S(2)}, u32[]{:S(2)}) %collective-permute-start.2) | collective-permute-done | bytes 524320 | tf_op jit(solution)/shard_map/ppermute | solution.py:18
  45.0 3.0 %collective-permute-start.5 = (bf16[128,2048]{1,0:T(8,128)(2,1)S(1)}, bf16[128,2048]{1,0:T(8,128)(2,1)S(1)}, u32[]{:S(2)}, u32[]{:S(2)}) collective-permute-start(bf16[128,2048]{1,0:T(8,128)(2,1)S(1)} %collective-permute-done.3), channel_id=1, source_target_pairs={{0,60},{4,0},{8,4},{12,8},{16,12},{20,16},{24,20},{28,24},{32,28},... | collective-permute-start | bytes 1572872 | tf_op jit(solution)/shard_map/ppermute | solution.py:23
  49.2 10.2 %all-to-all-start = ((bf16[64,1,32]{2,1,0:T(2,128)(2,1)}), bf16[64,1,32]{2,1,0:T(2,128)(2,1)S(1)}, u32[]{:S(2)}, u32[]{:S(2)}) async-start(bf16[64,1,32]{2,1,0:T(2,128)(2,1)} %broadcast_in_dim.7), calls=%async_computation | async-start | bytes 65536 | tf_op jit(solution)/shard_map/all_to_all | solution.py:32
  59.8 7.2 %collective-permute-done.4 = bf16[128,2048]{1,0:T(8,128)(2,1)S(1)} collective-permute-done((bf16[128,2048]{1,0:T(8,128)(2,1)}, bf16[128,2048]{1,0:T(8,128)(2,1)S(1)}, u32[]{:S(2)}, u32[]{:S(2)}) %collective-permute-start.4) | collective-permute-done | bytes 524320 | tf_op jit(solution)/shard_map/ppermute | solution.py:18
  66.9 4.5 %broadcast_in_dim.6 = bf16[2048,2048]{0,1:T(8,128)(2,1)} broadcast(bf16[]{:T(256)} %constant.91.clone.1), dimensions={} | broadcast | bytes 8388610 | tf_op jit(solution)/shard_map/broadcast_in_dim | solution.py:13
  73.0 1.3 copy.46
  74.3 3.0 %collective-permute-start.7 = (bf16[128,2048]{1,0:T(8,128)(2,1)S(1)}, bf16[128,2048]{1,0:T(8,128)(2,1)S(1)}, u32[]{:S(2)}, u32[]{:S(2)}) collective-permute-start(bf16[128,2048]{1,0:T(8,128)(2,1)S(1)} %collective-permute-done.5), channel_id=1, source_target_pairs={{0,60},{4,0},{8,4},{12,8},{16,12},{20,16},{24,20},{28,24},{32,28},... | collective-permute-start | bytes 1572872 | tf_op jit(solution)/shard_map/ppermute | solution.py:23
  79.2 1.3 copy.48
  80.6 4.6 %collective-permute-done.6 = bf16[128,2048]{1,0:T(8,128)(2,1)} collective-permute-done((bf16[128,2048]{1,0:T(8,128)(2,1)S(1)}, bf16[128,2048]{1,0:T(8,128)(2,1)}, u32[]{:S(2)}, u32[]{:S(2)}) %collective-permute-start.6) | collective-permute-done | bytes 524320 | tf_op jit(solution)/shard_map/ppermute | solution.py:18
  86.3 3.0 %collective-permute-start.9 = (bf16[128,2048]{1,0:T(8,128)(2,1)S(1)}, bf16[128,2048]{1,0:T(8,128)(2,1)}, u32[]{:S(2)}, u32[]{:S(2)}) collective-permute-start(bf16[128,2048]{1,0:T(8,128)(2,1)S(1)} %collective-permute-done.7), channel_id=1, source_target_pairs={{0,60},{4,0},{8,4},{12,8},{16,12},{20,16},{24,20},{28,24},{32,28},... | collective-permute-start | bytes 1572872 | tf_op jit(solution)/shard_map/ppermute | solution.py:23
  91.4 3.7 %collective-permute-done.8 = bf16[128,2048]{1,0:T(8,128)(2,1)S(1)} collective-permute-done((bf16[128,2048]{1,0:T(8,128)(2,1)}, bf16[128,2048]{1,0:T(8,128)(2,1)S(1)}, u32[]{:S(2)}, u32[]{:S(2)}) %collective-permute-start.8) | collective-permute-done | bytes 524320 | tf_op jit(solution)/shard_map/ppermute | solution.py:18
  96.0 1.3 copy.52
  97.3 3.0 %collective-permute-start.11 = (bf16[128,2048]{1,0:T(8,128)(2,1)}, bf16[128,2048]{1,0:T(8,128)(2,1)S(1)}, u32[]{:S(2)}, u32[]{:S(2)}) collective-permute-start(bf16[128,2048]{1,0:T(8,128)(2,1)} %collective-permute-done.9), channel_id=1, source_target_pairs={{0,60},{4,0},{8,4},{12,8},{16,12},{20,16},{24,20},{28,24},{32,28},... | collective-permute-start | bytes 1572872 | tf_op jit(solution)/shard_map/ppermute | solution.py:23
  102.5 2.5 %collective-permute-done.10 = bf16[128,2048]{1,0:T(8,128)(2,1)S(1)} collective-permute-done((bf16[128,2048]{1,0:T(8,128)(2,1)S(1)}, bf16[128,2048]{1,0:T(8,128)(2,1)S(1)}, u32[]{:S(2)}, u32[]{:S(2)}) %collective-permute-start.10) | collective-permute-done | bytes 524320 | tf_op jit(solution)/shard_map/ppermute | solution.py:18
  105.8 1.3 copy.55
  107.3 3.0 %collective-permute-start.13 = (bf16[128,2048]{1,0:T(8,128)(2,1)S(1)}, bf16[128,2048]{1,0:T(8,128)(2,1)S(1)}, u32[]{:S(2)}, u32[]{:S(2)}) collective-permute-start(bf16[128,2048]{1,0:T(8,128)(2,1)S(1)} %collective-permute-done.11), channel_id=1, source_target_pairs={{0,60},{4,0},{8,4},{12,8},{16,12},{20,16},{24,20},{28,24},{32,28},... | collective-permute-start | bytes 1572872 | tf_op jit(solution)/shard_map/ppermute | solution.py:23
  112.5 2.3 %collective-permute-done.12 = bf16[128,2048]{1,0:T(8,128)(2,1)S(1)} collective-permute-done((bf16[128,2048]{1,0:T(8,128)(2,1)S(1)}, bf16[128,2048]{1,0:T(8,128)(2,1)S(1)}, u32[]{:S(2)}, u32[]{:S(2)}) %collective-permute-start.12) | collective-permute-done | bytes 524320 | tf_op jit(solution)/shard_map/ppermute | solution.py:18
  119.0 5.7 %collective-permute-done.14 = bf16[128,2048]{1,0:T(8,128)(2,1)S(1)} collective-permute-done((bf16[128,2048]{1,0:T(8,128)(2,1)S(1)}, bf16[128,2048]{1,0:T(8,128)(2,1)S(1)}, u32[]{:S(2)}, u32[]{:S(2)}) %collective-permute-start.14) | collective-permute-done | bytes 524320 | tf_op jit(solution)/shard_map/ppermute | solution.py:18
  125.7 12.2 %copy.61 = bf16[2048,2048]{1,0:T(8,128)(2,1)} copy(bf16[2048,2048]{0,1:T(8,128)(2,1)} %bitcast.6) | data formatting | bytes 16777216
  (55 shorter events, 20.8 us)
Async XLA Ops:
  7.2 0.9 copy-start
  7.2 118.6 %all-gather.2.cloned.1.call-start = ((), (), s32[]{:S(2)}) async-start(), calls=%async_computation.1 | async-start | bytes 8912896 | tf_op jit(solution)/shard_map/all_gather | solution.py:56
  11.8 12.2 %collective-permute-start = (bf16[128,2048]{1,0:T(8,128)(2,1)S(1)}, bf16[128,2048]{1,0:T(8,128)(2,1)S(1)}, u32[]{:S(2)}, u32[]{:S(2)}) collective-permute-start(bf16[128,2048]{1,0:T(8,128)(2,1)S(1)} %fusion.3), channel_id=1, source_target_pairs={{0,4},{4,8},{8,12},{12,16},{16,20},{20,24},{24,28},{28,32},{32,36}... | collective-permute-start | bytes 1572872 | tf_op jit(solution)/shard_map/ppermute | solution.py:18
  11.8 12.2 %collective-permute-start.1 = (bf16[128,2048]{1,0:T(8,128)(2,1)S(1)}, bf16[128,2048]{1,0:T(8,128)(2,1)S(1)}, u32[]{:S(2)}, u32[]{:S(2)}) collective-permute-start(bf16[128,2048]{1,0:T(8,128)(2,1)S(1)} %fusion.3), channel_id=1, source_target_pairs={{0,60},{4,0},{8,4},{12,8},{16,12},{20,16},{24,20},{28,24},{32,28},... | collective-permute-start | bytes 1572872 | tf_op jit(solution)/shard_map/ppermute | solution.py:23
  24.0 3.0 %copy-start.1 = (bf16[128,2048]{1,0:T(8,128)(2,1)}, bf16[128,2048]{1,0:T(8,128)(2,1)S(1)}, u32[]{:S(2)}) copy-start(bf16[128,2048]{1,0:T(8,128)(2,1)S(1)} %collective-permute-done) | copy-start | bytes 1572868
  24.0 21.0 %collective-permute-start.2 = (bf16[128,2048]{1,0:T(8,128)(2,1)S(1)}, bf16[128,2048]{1,0:T(8,128)(2,1)}, u32[]{:S(2)}, u32[]{:S(2)}) collective-permute-start(bf16[128,2048]{1,0:T(8,128)(2,1)S(1)} %collective-permute-done), channel_id=1, source_target_pairs={{0,4},{4,8},{8,12},{12,16},{16,20},{20,24},{24,28},{28,32},{32,36}... | collective-permute-start | bytes 1572872 | tf_op jit(solution)/shard_map/ppermute | solution.py:18
  24.0 21.0 %collective-permute-start.3 = (bf16[128,2048]{1,0:T(8,128)(2,1)S(1)}, bf16[128,2048]{1,0:T(8,128)(2,1)S(1)}, u32[]{:S(2)}, u32[]{:S(2)}) collective-permute-start(bf16[128,2048]{1,0:T(8,128)(2,1)S(1)} %collective-permute-done.1), channel_id=1, source_target_pairs={{0,60},{4,0},{8,4},{12,8},{16,12},{20,16},{24,20},{28,24},{32,28},... | collective-permute-start | bytes 1572872 | tf_op jit(solution)/shard_map/ppermute | solution.py:23
  45.0 21.9 %collective-permute-start.4 = (bf16[128,2048]{1,0:T(8,128)(2,1)}, bf16[128,2048]{1,0:T(8,128)(2,1)S(1)}, u32[]{:S(2)}, u32[]{:S(2)}) collective-permute-start(bf16[128,2048]{1,0:T(8,128)(2,1)} %collective-permute-done.2), channel_id=1, source_target_pairs={{0,4},{4,8},{8,12},{12,16},{16,20},{20,24},{24,28},{28,32},{32,36}... | collective-permute-start | bytes 1572872 | tf_op jit(solution)/shard_map/ppermute | solution.py:18
  45.0 29.3 %collective-permute-start.5 = (bf16[128,2048]{1,0:T(8,128)(2,1)S(1)}, bf16[128,2048]{1,0:T(8,128)(2,1)S(1)}, u32[]{:S(2)}, u32[]{:S(2)}) collective-permute-start(bf16[128,2048]{1,0:T(8,128)(2,1)S(1)} %collective-permute-done.3), channel_id=1, source_target_pairs={{0,60},{4,0},{8,4},{12,8},{16,12},{20,16},{24,20},{28,24},{32,28},... | collective-permute-start | bytes 1572872 | tf_op jit(solution)/shard_map/ppermute | solution.py:23
  49.2 23.0 %all-to-all-start = ((bf16[64,1,32]{2,1,0:T(2,128)(2,1)}), bf16[64,1,32]{2,1,0:T(2,128)(2,1)S(1)}, u32[]{:S(2)}, u32[]{:S(2)}) async-start(bf16[64,1,32]{2,1,0:T(2,128)(2,1)} %broadcast_in_dim.7), calls=%async_computation | async-start | bytes 65536 | tf_op jit(solution)/shard_map/all_to_all | solution.py:32
  66.9 18.2 %collective-permute-start.6 = (bf16[128,2048]{1,0:T(8,128)(2,1)S(1)}, bf16[128,2048]{1,0:T(8,128)(2,1)}, u32[]{:S(2)}, u32[]{:S(2)}) collective-permute-start(bf16[128,2048]{1,0:T(8,128)(2,1)S(1)} %collective-permute-done.4), channel_id=1, source_target_pairs={{0,4},{4,8},{8,12},{12,16},{16,20},{20,24},{24,28},{28,32},{32,36}... | collective-permute-start | bytes 1572872 | tf_op jit(solution)/shard_map/ppermute | solution.py:18
  74.3 11.9 %collective-permute-start.7 = (bf16[128,2048]{1,0:T(8,128)(2,1)S(1)}, bf16[128,2048]{1,0:T(8,128)(2,1)S(1)}, u32[]{:S(2)}, u32[]{:S(2)}) collective-permute-start(bf16[128,2048]{1,0:T(8,128)(2,1)S(1)} %collective-permute-done.5), channel_id=1, source_target_pairs={{0,60},{4,0},{8,4},{12,8},{16,12},{20,16},{24,20},{28,24},{32,28},... | collective-permute-start | bytes 1572872 | tf_op jit(solution)/shard_map/ppermute | solution.py:23
  85.1 10.0 %collective-permute-start.8 = (bf16[128,2048]{1,0:T(8,128)(2,1)}, bf16[128,2048]{1,0:T(8,128)(2,1)S(1)}, u32[]{:S(2)}, u32[]{:S(2)}) collective-permute-start(bf16[128,2048]{1,0:T(8,128)(2,1)} %collective-permute-done.6), channel_id=1, source_target_pairs={{0,4},{4,8},{8,12},{12,16},{16,20},{20,24},{24,28},{28,32},{32,36}... | collective-permute-start | bytes 1572872 | tf_op jit(solution)/shard_map/ppermute | solution.py:18
  86.3 11.1 %collective-permute-start.9 = (bf16[128,2048]{1,0:T(8,128)(2,1)S(1)}, bf16[128,2048]{1,0:T(8,128)(2,1)}, u32[]{:S(2)}, u32[]{:S(2)}) collective-permute-start(bf16[128,2048]{1,0:T(8,128)(2,1)S(1)} %collective-permute-done.7), channel_id=1, source_target_pairs={{0,60},{4,0},{8,4},{12,8},{16,12},{20,16},{24,20},{28,24},{32,28},... | collective-permute-start | bytes 1572872 | tf_op jit(solution)/shard_map/ppermute | solution.py:23
  95.2 9.8 %collective-permute-start.10 = (bf16[128,2048]{1,0:T(8,128)(2,1)S(1)}, bf16[128,2048]{1,0:T(8,128)(2,1)S(1)}, u32[]{:S(2)}, u32[]{:S(2)}) collective-permute-start(bf16[128,2048]{1,0:T(8,128)(2,1)S(1)} %collective-permute-done.8), channel_id=1, source_target_pairs={{0,4},{4,8},{8,12},{12,16},{16,20},{20,24},{24,28},{28,32},{32,36}... | collective-permute-start | bytes 1572872 | tf_op jit(solution)/shard_map/ppermute | solution.py:18
  97.3 10.0 %collective-permute-start.11 = (bf16[128,2048]{1,0:T(8,128)(2,1)}, bf16[128,2048]{1,0:T(8,128)(2,1)S(1)}, u32[]{:S(2)}, u32[]{:S(2)}) collective-permute-start(bf16[128,2048]{1,0:T(8,128)(2,1)} %collective-permute-done.9), channel_id=1, source_target_pairs={{0,60},{4,0},{8,4},{12,8},{16,12},{20,16},{24,20},{28,24},{32,28},... | collective-permute-start | bytes 1572872 | tf_op jit(solution)/shard_map/ppermute | solution.py:23
  105.0 9.8 %collective-permute-start.12 = (bf16[128,2048]{1,0:T(8,128)(2,1)S(1)}, bf16[128,2048]{1,0:T(8,128)(2,1)S(1)}, u32[]{:S(2)}, u32[]{:S(2)}) collective-permute-start(bf16[128,2048]{1,0:T(8,128)(2,1)S(1)} %collective-permute-done.10), channel_id=1, source_target_pairs={{0,4},{4,8},{8,12},{12,16},{16,20},{20,24},{24,28},{28,32},{32,36}... | collective-permute-start | bytes 1572872 | tf_op jit(solution)/shard_map/ppermute | solution.py:18
  107.3 9.7 %collective-permute-start.13 = (bf16[128,2048]{1,0:T(8,128)(2,1)S(1)}, bf16[128,2048]{1,0:T(8,128)(2,1)S(1)}, u32[]{:S(2)}, u32[]{:S(2)}) collective-permute-start(bf16[128,2048]{1,0:T(8,128)(2,1)S(1)} %collective-permute-done.11), channel_id=1, source_target_pairs={{0,60},{4,0},{8,4},{12,8},{16,12},{20,16},{24,20},{28,24},{32,28},... | collective-permute-start | bytes 1572872 | tf_op jit(solution)/shard_map/ppermute | solution.py:23
  114.8 9.8 %collective-permute-start.14 = (bf16[128,2048]{1,0:T(8,128)(2,1)S(1)}, bf16[128,2048]{1,0:T(8,128)(2,1)S(1)}, u32[]{:S(2)}, u32[]{:S(2)}) collective-permute-start(bf16[128,2048]{1,0:T(8,128)(2,1)S(1)} %collective-permute-done.12), channel_id=1, source_target_pairs={{0,4},{4,8},{8,12},{12,16},{16,20},{20,24},{24,28},{28,32},{32,36}... | collective-permute-start | bytes 1572872 | tf_op jit(solution)/shard_map/ppermute | solution.py:18
Sparse Core Ops, SparseCore 0:
  10.4 74.7 all-gather.1
